TPU v7x, 256 devices: a whole 4x4x8 slice. The times are simulated.
256 devices in a mesh: batch: 4 (over z_lo), grid: 64 (over x, y, z_hi, core).
Axes of the slice: x: 4, y: 4, z: 8 (z_hi: 2, z_lo: 4; z = z_hi * 4 + z_lo), core: 2. Of those that a mesh axis runs over, the one named last changes fastest.
Arguments:
- fields: bfloat16 [1024, 512, 512], P(('batch', 'grid')), parts along dimension 0, may hold values from -18 to 18
- norm_gain: float32 [256], replicated, may hold values from 0.5 to 1.5
- norm_shift: float32 [256], replicated, may hold values from -3 to 3
- first_weight: bfloat16 [2, 8, 32, 32], replicated, may hold values from -0.75 to 0.75
- second_weight: bfloat16 [2, 8, 32, 32], replicated, may hold values from -0.75 to 0.75
- first_bias: float32 [2, 256], replicated, may hold values from -2 to 2
Outputs:
- mixed_fields: bfloat16 [1024, 512, 512], P(('batch', 'grid')), parts along dimension 0
There are 4 independent parts, one for each index of `batch`. A program takes and returns all parts, laid end to end along the dimension named above; an argument that names none is the same for every part. Nothing has to cross between parts.
All inputs are finite; a program needn't handle non-finite values.
Results may differ from a plain program's by a relative error of at most 0.0055.
Values may be sent and summed in bfloat16 or wider, within the bound.
A program may use at most 64 MiB of HBM per device.

v0:
```python
import functools
import math

import jax
import jax.numpy as jnp
import ml_dtypes
import numpy as np
from jax import lax
from jax.experimental import pallas as pl
from jax.experimental.pallas import tpu as pltpu
from jax.sharding import PartitionSpec as P

MESH = pl.DeviceIdType.MESH
BF = jnp.bfloat16
F32 = jnp.float32
N = 512
ROWS = 128
RS = 40
SS = 520
KB = 16


def tables():
    half = N // 2
    idx = np.arange(N)
    step = np.float32(2.0 * math.pi / N)
    scale = np.float32(1.0 / math.sqrt(N))
    angle_w = ((idx[:, None] * np.arange(half)[None, :]) % N).astype(np.float32) * step
    cos_w, sin_w = np.cos(angle_w), np.sin(angle_w)
    weight = np.where(np.arange(half) == 0, 1.0, 2.0).astype(np.float32)
    re, im = cos_w * scale, -sin_w * scale
    fwd = np.stack(
        [np.concatenate([re[:, s], im[:, s]], 1) for s in (slice(0, 128), slice(128, 256))]
    )
    ire, iim = (cos_w * weight * scale).T, (-sin_w * weight * scale).T
    inv = np.stack(
        [np.concatenate([ire[s], iim[s]], 0) for s in (slice(0, 128), slice(128, 256))]
    )
    angle_h = ((idx[:, None] * idx[None, :]) % N).astype(np.float32) * step
    both = np.concatenate([np.cos(angle_h) * scale, np.sin(angle_h) * scale], 1)
    cast = lambda a: a.astype(ml_dtypes.bfloat16)
    return cast(fwd), cast(inv), cast(both)


def kernel(
    f_hbm, gain, shift, w1, w2, bias, fwd_hbm, inv_hbm, both_hbm,
    out_hbm,
    fld, mode_re, mode_im, shr_re, shr_im, stat, part, xbuf, xsum, ybuf, ysum, zbuf,
    fwd_t, inv_t, both_t, big1, big2, bcol, stack, back_own, back_out, back_in, out_v,
    zs, zr, ys, yr, ds, dr, os, orr, cys, cyr, czs, czr, cds, cdr,
    xs1, xr1, ys1, yr1, zs1, zr1, ys2, yr2, xs2, xr2, cs2, cr2, bs, br, loc, tab, outs,
):
    b = lax.axis_index("batch")
    g = lax.axis_index("grid")
    core = lax.rem(g, 2)
    zh = lax.rem(lax.div(g, 2), 2)
    y = lax.rem(lax.div(g, 4), 4)
    x = lax.div(g, 16)
    yy = lax.rem(y, 2)
    blk = lax.div(g, 8)

    def dev(x_, y_, z_, c_):
        return (b, ((x_ * 4 + y_) * 2 + z_) * 2 + c_)

    def flip(v, d):
        return v + d - 2 * v * d

    def base(dy, dz, dc):
        return ((flip(yy, dy) * 2 + flip(zh, dz)) * 2 + flip(core, dc)) * 4

    ypart = dev(x, y + 1 - 2 * yy, zh, core)
    zpart = dev(x, y, 1 - zh, core)
    cpart = dev(x, y, zh, 1 - core)
    xpeer = [lax.rem(x + 4 - d, 4) for d in (1, 2, 3)]
    ypeer = [lax.rem(y + 4 - d, 4) for d in (1, 2, 3)]
    xdev = [dev(v, y, zh, core) for v in xpeer]
    ydev = [dev(x, v, zh, core) for v in ypeer]

    def remote(src, dst, send, recv, to):
        return pltpu.make_async_remote_copy(
            src_ref=src, dst_ref=dst, send_sem=send, recv_sem=recv, device_id=to, device_id_type=MESH
        )

    own = base(0, 0, 0)
    tabs = [
        pltpu.make_async_copy(fwd_hbm.at[core], fwd_t, tab.at[0]),
        pltpu.make_async_copy(inv_hbm, inv_t, tab.at[1]),
        pltpu.make_async_copy(both_hbm, both_t, tab.at[2]),
    ]
    fetch = [pltpu.make_async_copy(f_hbm.at[i], fld.at[own + i], loc.at[i]) for i in range(4)]
    for c in fetch:
        c.start()

    barrier = pltpu.get_barrier_semaphore()
    peers = xdev + ydev + [zpart, cpart]
    for p in peers:
        pl.semaphore_signal(barrier, inc=1, device_id=p, device_id_type=MESH)
    pl.semaphore_wait(barrier, len(peers))
    for c in fetch:
        c.wait()
    for c in tabs:
        c.start()

    def piece(first, n):
        row = pl.multiple_of((n % 4) * ROWS, ROWS)
        return fld.at[first + n // 4, pl.ds(row, ROWS), :]

    def same(ref, send, recv, to):
        return remote(ref, ref, send, recv, to)

    def zchunk(n):
        return same(piece(own, n), zs.at[0], zr.at[n], zpart)

    def ychunk(n):
        return same(piece(own, n), ys.at[0], yr.at[n], ypart)

    def dchunk(n):
        return same(piece(base(0, 1, 0), n), ds.at[0], dr.at[n], ypart)

    def cychunk(n):
        return same(piece(base(1, 0, 0), n), cys.at[0], cyr.at[n], cpart)

    def czchunk(n):
        return same(piece(base(0, 1, 0), n), czs.at[0], czr.at[n], cpart)

    def cdchunk(n):
        return same(piece(base(1, 1, 0), n), cds.at[0], cdr.at[n], cpart)

    def owncopy(i, h):
        rows = pl.ds(pl.multiple_of(256 * h, 256), 256)
        return fld.at[own + i, rows, :]

    ownc = [same(owncopy(i, 1 - core), os.at[0], orr.at[i], cpart) for i in range(4)]
    ownc += [same(owncopy(i, core), os.at[0], orr.at[4 + i], cpart) for i in range(4)]
    for c in ownc[:4]:
        c.start()
    for n in range(3):
        zchunk(n).start()
    for n in range(5):
        ychunk(n).start()
    for c in ownc[4:]:
        c.start()

    for c in ownc[:4]:
        c.wait_recv()
    other = base(0, 0, 1)

    def partial_sums(r, _):
        row = pl.multiple_of(256 * core + r * 16, 16)
        s1 = jnp.zeros((16, N), F32)
        s2 = jnp.zeros((16, N), F32)
        for first in (own, other):
            for i in range(4):
                v = fld[first + i, pl.ds(row, 16), :].astype(F32)
                s1 = s1 + v
                s2 = s2 + v * v
        at = pl.ds(pl.multiple_of(r * 16, 16), 16)
        part[0, at, :] = s1
        part[1, at, :] = s2
        return 0

    lax.fori_loop(0, 16, partial_sums, 0)

    xrs = [
        remote(
            part.at[:, pl.ds(pl.multiple_of(64 * xpeer[d], 64), 64), :],
            xbuf.at[d], xs1.at[d], xr1.at[d], xdev[d],
        )
        for d in range(3)
    ]
    for c in xrs:
        c.start()

    for c in tabs:
        c.wait()

    def iota(shape, dim):
        return lax.broadcasted_iota(jnp.int32, shape, dim)

    pick = (iota((256, 32), 0) % 32 == iota((256, 32), 1)).astype(BF)
    nt = (((1,), (1,)), ((), ()))

    def expand(rows, w, sel):
        left = lax.dot_general(sel, w, nt, preferred_element_type=F32).astype(BF)
        return lax.dot_general(left, pick, nt, preferred_element_type=F32)

    def complex_matrix(rows, per, sel, w):
        t0 = expand(rows, w[0, blk], sel)
        t1 = expand(rows, w[1, blk], sel)
        r = iota((rows, 256), 0)
        c = iota((rows, 256), 1)
        rp, cp = r // (4 * per), c // 128
        hit = (r // per) % 4 == (c // 32) % 4
        val = jnp.where(rp == cp, t0, jnp.where(rp == 1, t1, -t1))
        return jnp.where(hit, val, 0.0).astype(BF)

    big1[...] = complex_matrix(256, 32, pick, w1)
    chip = yy * 2 + zh
    pick2 = ((iota((64, 32), 0) % 8) + chip * 8 == iota((64, 32), 1)).astype(BF)
    big2[...] = complex_matrix(64, 8, pick2, w2)
    r = iota((256, 256), 0)
    c = iota((256, 256), 1)
    hit = (r % 32) + blk * 32 == c
    value = jnp.where(r < 128, bias[0:1, :], bias[1:2, :])
    col = jnp.sum(jnp.where(hit, value, 0.0), axis=1, keepdims=True)
    bcol[...] = jnp.broadcast_to(col, (256, 128))

    for c in xrs:
        c.wait_recv()
    mine = pl.ds(pl.multiple_of(64 * x, 64), 64)
    xsum[...] = part[:, mine, :] + xbuf[0] + xbuf[1] + xbuf[2]
    yrs = [
        remote(
            xsum.at[:, pl.ds(pl.multiple_of(16 * ypeer[d], 16), 16), :],
            ybuf.at[d], ys1.at[d], yr1.at[d], ydev[d],
        )
        for d in range(3)
    ]
    for c in yrs:
        c.start()
    for n in range(5, 8):
        ychunk(n).start()
    for c in yrs:
        c.wait_recv()
    mine = pl.ds(pl.multiple_of(16 * y, 16), 16)
    ysum[...] = xsum[:, mine, :] + ybuf[0] + ybuf[1] + ybuf[2]
    zex = remote(ysum, zbuf, zs1.at[0], zr1.at[0], zpart)
    zex.start()
    for n in range(3, 16):
        zchunk(n).start()
    zex.wait_recv()
    total = ysum[...] + zbuf[...]
    mean = total[0] * (1.0 / 256.0)
    var = total[1] * (1.0 / 256.0) - mean * mean
    row0 = 256 * core + 64 * x
    mine = pl.ds(pl.multiple_of(row0 + 16 * y, 16), 16)
    stat[0, mine, :] = mean
    stat[1, mine, :] = lax.rsqrt(var + 1e-5)
    yag = [same(stat.at[:, mine, :], ys2.at[d], yr2.at[d], ydev[d]) for d in range(3)]
    for c in yag:
        c.start()
    for n in range(8, 16):
        ychunk(n).start()
    for c in yag:
        c.wait_recv()
    mine = pl.ds(pl.multiple_of(row0, 64), 64)
    xag = [same(stat.at[:, mine, :], xs2.at[d], xr2.at[d], xdev[d]) for d in range(3)]
    for c in xag:
        c.start()

    def forward_z(n):
        zchunk(n).wait_recv()
        dchunk(n).start()
        czchunk(n).start()

    def forward_y(n):
        ychunk(n).wait_recv()
        cychunk(n).start()

    def forward_d(n):
        dchunk(n).wait_recv()
        cdchunk(n).start()

    for n in range(5):
        forward_z(n)
        forward_y(n)
    for c in xag:
        c.wait_recv()
    mine = pl.ds(pl.multiple_of(256 * core, 256), 256)
    cag = same(stat.at[:, mine, :], cs2.at[0], cr2.at[0], cpart)
    cag.start()
    for n in range(5, 8):
        forward_z(n)
        forward_y(n)
    cag.wait_recv()
    for c in ownc[4:]:
        c.wait_recv()

    def forward(slot):
        gn = gain[blk * 32 + slot]
        sh = shift[blk * 32 + slot]
        for h in range(0, N, 128):
            rows = slice(h, h + 128)
            v = fld[slot, rows, :].astype(F32)
            nrm = ((v - stat[0, rows, :]) * stat[1, rows, :] * gn + sh).astype(BF)
            a = jnp.dot(nrm, fwd_t[...], preferred_element_type=F32)
            stack[h : h + 128, :] = a.astype(BF)
            stack[N + h : N + h + 128, :] = jnp.concatenate([a[:, 128:], -a[:, :128]], 1).astype(BF)
        m = jnp.dot(both_t[...], stack[...], preferred_element_type=F32)
        mode_re[pl.ds(slot, N, stride=RS), :] = m[:, :128]
        mode_im[pl.ds(slot, N, stride=RS), :] = m[:, 128:]

    def step(t, _):
        @pl.when(t < 2)
        def _():
            for k in range(4):
                forward_y(8 + 4 * t + k)

        forward_z(8 + t)
        for k in range(2):
            forward_d(2 * t + k)

        @pl.when(t == 3)
        def _():
            for n in range(16):
                cychunk(n).wait_recv()

        @pl.when(t == 4)
        def _():
            for n in range(8):
                czchunk(n).wait_recv()

        @pl.when(t == 5)
        def _():
            for n in range(8):
                cdchunk(n).wait_recv()

        @pl.when(t == 6)
        def _():
            for n in range(8, 12):
                czchunk(n).wait_recv()
                cdchunk(n).wait_recv()

        @pl.when(t == 7)
        def _():
            for n in range(12, 16):
                czchunk(n).wait_recv()
                cdchunk(n).wait_recv()

        def one(e, _):
            lo, hi = lax.rem(e, 2), lax.div(e, 2)
            early = t < 4
            late = t > 5
            dy = jnp.where(early, lax.div(t, 2), jnp.where(late, hi, t - 4))
            dz = jnp.where(early, 0, 1)
            dc = jnp.where(early, lax.rem(t, 2), lo)
            i = jnp.where(early, e, jnp.where(late, t - 4, hi))
            forward(base(dy, dz, dc) + i)
            return 0

        lax.fori_loop(0, 4, one, 0)
        return 0

    lax.fori_loop(0, 8, step, 0)

    groups = KB // 4

    def mix(t, _):
        def cols(ref):
            return [
                jnp.concatenate(
                    [
                        ref[pl.ds(pl.multiple_of((t * KB + q * 4 + k) * RS, 8), 32), :]
                        for k in range(4)
                    ],
                    0,
                )
                for q in range(groups)
            ]

        re, im = cols(mode_re), cols(mode_im)
        z = jnp.concatenate(
            [jnp.concatenate([re[q], im[q]], 0) for q in range(groups)], 1
        ).astype(BF)
        hid = jnp.dot(big1[...], z, preferred_element_type=F32)
        hid = jnp.maximum(hid + jnp.concatenate([bcol[...]] * groups, 1), 0.0).astype(BF)
        o = jnp.dot(big2[...], hid, preferred_element_type=F32)
        o = jnp.maximum(o - 0.01, 0.0) + jnp.minimum(o + 0.01, 0.0)
        for q in range(groups):
            for k in range(4):
                at = pl.ds(t * KB + q * 4 + k, 8, stride=SS)
                shr_re[at, :] = o[k * 8 : k * 8 + 8, q * 128 : q * 128 + 128]
                shr_im[at, :] = o[32 + k * 8 : 40 + k * 8, q * 128 : q * 128 + 128]
        return 0

    lax.fori_loop(0, N // KB, mix, 0)

    def backward(c8):
        at = pl.ds(pl.multiple_of(c8 * SS, 8), N)
        sr, si = shr_re[at, :], shr_im[at, :]
        stack[0:N, :] = jnp.concatenate([sr, si], 1).astype(BF)
        stack[N : 2 * N, :] = jnp.concatenate([-si, sr], 1).astype(BF)
        return jnp.dot(both_t[...], stack[...], preferred_element_type=F32).astype(BF)

    def swap(i):
        return remote(back_out.at[i], back_in.at[i], bs.at[i], br.at[i], cpart)

    def give(i, _):
        back_out[i] = backward((1 - core) * 4 + i)
        swap(i).start()
        return 0

    def keep(i, _):
        back_own[i] = backward(core * 4 + i)
        return 0

    def put(i):
        return pltpu.make_async_copy(out_v.at[i], out_hbm.at[i], outs.at[i])

    def finish(i, _):
        swap(i).wait_recv()
        filt = jnp.dot(back_own[i], inv_t[core], preferred_element_type=F32)
        filt = filt + jnp.dot(back_in[i], inv_t[1 - core], preferred_element_type=F32)
        out_v[i] = (fld[own + i].astype(F32) + filt).astype(BF)
        put(i).start()
        return 0

    lax.fori_loop(0, 4, give, 0)
    lax.fori_loop(0, 4, keep, 0)
    lax.fori_loop(0, 4, finish, 0)

    def drain(first, send, to):
        ref = fld.at[pl.ds(first, 4)]
        same(ref, send, zr.at[0], to).wait_send()

    drain(own, zs.at[0], zpart)
    drain(own, ys.at[0], ypart)
    drain(own, os.at[0], cpart)
    drain(base(0, 1, 0), ds.at[0], ypart)
    drain(base(1, 0, 0), cys.at[0], cpart)
    drain(base(0, 1, 0), czs.at[0], cpart)
    drain(base(1, 1, 0), cds.at[0], cpart)
    for c in xrs + yrs + [zex] + yag + xag + [cag]:
        c.wait_send()
    for i in range(4):
        swap(i).wait_send()
        put(i).wait()


def per_device(fields, norm_gain, norm_shift, first_weight, second_weight, first_bias):
    fwd, inv, both = tables()
    dma = pltpu.SemaphoreType.DMA
    vm, sm, hbm = pltpu.VMEM, pltpu.SMEM, pl.ANY
    spec = lambda s: pl.BlockSpec(memory_space=s)
    return pl.pallas_call(
        kernel,
        out_shape=jax.ShapeDtypeStruct((4, N, N), BF),
        in_specs=[spec(s) for s in (hbm, sm, sm, vm, vm, vm, hbm, hbm, hbm)],
        out_specs=spec(hbm),
        scratch_shapes=[
            vm((32, N, N), BF),
            vm((N * RS, 128), F32),
            vm((N * RS, 128), F32),
            vm((8 * SS, 128), F32),
            vm((8 * SS, 128), F32),
            vm((2, N, N), F32),
            vm((2, 256, N), F32),
            vm((3, 2, 64, N), F32),
            vm((2, 64, N), F32),
            vm((3, 2, 16, N), F32),
            vm((2, 16, N), F32),
            vm((2, 16, N), F32),
            vm((N, 256), BF),
            vm((2, 256, N), BF),
            vm((N, 2 * N), BF),
            vm((256, 256), BF),
            vm((64, 256), BF),
            vm((256, 128), F32),
            vm((2 * N, 256), BF),
            vm((4, N, 256), BF),
            vm((4, N, 256), BF),
            vm((4, N, 256), BF),
            vm((4, N, N), BF),
        ]
        + [
            dma((n,))
            for n in (
                1, 16, 1, 16, 1, 16, 1, 8, 1, 16, 1, 16, 1, 16,
                3, 3, 3, 3, 1, 1, 3, 3, 3, 3, 1, 1, 4, 4, 4, 3, 4,
            )
        ],
        compiler_params=pltpu.CompilerParams(
            collective_id=0, has_side_effects=True, vmem_limit_bytes=67043328
        ),
        name="afno",
    )(fields, norm_gain, norm_shift, first_weight, second_weight, first_bias, fwd, inv, both)


def solution(mesh):
    return jax.shard_map(
        per_device,
        mesh=mesh,
        in_specs=(P(("batch", "grid"), None, None), P(), P(), P(), P(), P()),
        out_specs=P(("batch", "grid"), None, None),
        check_vma=False,
    )
```

profile of v0, /device:TPU:33, one launch (start us, length us, event | category | flops | bytes accessed | tf_op | source)
XLA Modules:
  0.0 144.4 jit_solution(18329727913883716606)
XLA Ops:
  0.0 141.3 %afno.1 = bf16[4,512,512]{2,1,0:T(8,128)(2,1)} custom-call(bf16[4,512,512]{2,1,0:T(8,128)(2,1)} %f_hbm.1, f32[256]{0:T(256)} %gain.1, f32[256]{0:T(256)} %shift.1, bf16[2,8,32,32]{3,2,1,0:T(8,128)(2,1)} %w1.1, bf16[2,8,32,32]{3,2,1,0:T(8,128)(2,1)} %w2.1, f32[2,256]{1,0:T(2,128)} %bias.1, bf16[2,512,256]{2,1,0:T(8,128)(2,1)} %constant.6.clone.fwd_hbm, ...), custom_call_target="tpu_custom_call" | custom-call | tf_op jit(solution)/shard_map/afno/pallas_call | solution.py:435
  141.3 3.0 %copy.11 = bf16[4,512,512]{2,1,0:T(8,128)(2,1)} copy(bf16[4,512,512]{2,1,0:T(8,128)(2,1)} %afno.1) | data formatting | bytes 4194304
where the time goes:
time: 145 us; the launch traced here: 144 us
  Pallas kernels  141 us (97%)
  local copies, waits for them, and re-layouts  3.05 us (2%)
    pallas_call x1, Pallas kernels, per_device(): pl.pallas_call(kernel, out_shape=jax.ShapeDtypeStruct((4, N, N), BF), in_...  141 us
    unnamed x1, local copies, waits for them, and re-layouts  3.05 us

commit v1 on v0

--- a/solution.py
+++ b/solution.py
@@ -17,7 +17,11 @@
 ROWS = 128
 RS = 40
 SS = 520
-KB = 16
+KB = 64
+
+
+ZA = 8
+YB = 4
 
 
 def tables():
@@ -105,14 +109,18 @@
         row = pl.multiple_of((n % 4) * ROWS, ROWS)
         return fld.at[first + n // 4, pl.ds(row, ROWS), :]
 
+    def half(first, n):
+        row = pl.multiple_of((n % 8) * 64, 64)
+        return fld.at[first + n // 8, pl.ds(row, 64), :]
+
     def same(ref, send, recv, to):
         return remote(ref, ref, send, recv, to)
 
     def zchunk(n):
-        return same(piece(own, n), zs.at[0], zr.at[n], zpart)
+        return same(half(own, n), zs.at[n], zr.at[n], zpart)
 
     def ychunk(n):
-        return same(piece(own, n), ys.at[0], yr.at[n], ypart)
+        return same(half(own, n), ys.at[n], yr.at[n], ypart)
 
     def dchunk(n):
         return same(piece(base(0, 1, 0), n), ds.at[0], dr.at[n], ypart)
@@ -134,10 +142,14 @@
     ownc += [same(owncopy(i, core), os.at[0], orr.at[4 + i], cpart) for i in range(4)]
     for c in ownc[:4]:
         c.start()
-    for n in range(3):
-        zchunk(n).start()
-    for n in range(5):
-        ychunk(n).start()
+    def pump(chunk, first, last):
+        for n in range(first, last):
+            if n > 1:
+                chunk(n - 2).wait_send()
+            chunk(n).start()
+
+    pump(zchunk, 0, 2)
+    pump(ychunk, 0, 2)
     for c in ownc[4:]:
         c.start()
 
@@ -205,6 +217,9 @@
     col = jnp.sum(jnp.where(hit, value, 0.0), axis=1, keepdims=True)
     bcol[...] = jnp.broadcast_to(col, (256, 128))
 
+    for n in range(2, ZA):
+        pump(ychunk, 2 * n - 2, 2 * n)
+        pump(zchunk, n, n + 1)
     for c in xrs:
         c.wait_recv()
     mine = pl.ds(pl.multiple_of(64 * x, 64), 64)
@@ -218,16 +233,19 @@
     ]
     for c in yrs:
         c.start()
-    for n in range(5, 8):
-        ychunk(n).start()
+    for c in yrs:
+        c.wait_send()
+    pump(ychunk, 2 * ZA - 2, 2 * ZA)
+    pump(zchunk, ZA, ZA + 1)
     for c in yrs:
         c.wait_recv()
     mine = pl.ds(pl.multiple_of(16 * y, 16), 16)
     ysum[...] = xsum[:, mine, :] + ybuf[0] + ybuf[1] + ybuf[2]
     zex = remote(ysum, zbuf, zs1.at[0], zr1.at[0], zpart)
     zex.start()
-    for n in range(3, 16):
-        zchunk(n).start()
+    pump(ychunk, 2 * ZA, 2 * ZA + YB)
+    zex.wait_send()
+    pump(zchunk, ZA + 1, ZA + 3)
     zex.wait_recv()
     total = ysum[...] + zbuf[...]
     mean = total[0] * (1.0 / 256.0)
@@ -239,22 +257,30 @@
     yag = [same(stat.at[:, mine, :], ys2.at[d], yr2.at[d], ydev[d]) for d in range(3)]
     for c in yag:
         c.start()
-    for n in range(8, 16):
-        ychunk(n).start()
+    for c in yag:
+        c.wait_send()
+    pump(zchunk, ZA + 3, ZA + 4)
+    pump(ychunk, 2 * ZA + YB, 2 * ZA + YB + 2)
     for c in yag:
         c.wait_recv()
     mine = pl.ds(pl.multiple_of(row0, 64), 64)
     xag = [same(stat.at[:, mine, :], xs2.at[d], xr2.at[d], xdev[d]) for d in range(3)]
     for c in xag:
         c.start()
+    for n in range(ZA + 4, 32):
+        zchunk(n).start()
+    for n in range(2 * ZA + YB + 2, 32):
+        ychunk(n).start()
 
     def forward_z(n):
-        zchunk(n).wait_recv()
+        zchunk(2 * n).wait_recv()
+        zchunk(2 * n + 1).wait_recv()
         dchunk(n).start()
         czchunk(n).start()
 
     def forward_y(n):
-        ychunk(n).wait_recv()
+        ychunk(2 * n).wait_recv()
+        ychunk(2 * n + 1).wait_recv()
         cychunk(n).start()
 
     def forward_d(n):
@@ -413,14 +439,16 @@
         ref = fld.at[pl.ds(first, 4)]
         same(ref, send, zr.at[0], to).wait_send()
 
-    drain(own, zs.at[0], zpart)
-    drain(own, ys.at[0], ypart)
+    for n in range(ZA + 2, 32):
+        zchunk(n).wait_send()
+    for n in range(2 * ZA + YB, 32):
+        ychunk(n).wait_send()
     drain(own, os.at[0], cpart)
     drain(base(0, 1, 0), ds.at[0], ypart)
     drain(base(1, 0, 0), cys.at[0], cpart)
     drain(base(0, 1, 0), czs.at[0], cpart)
     drain(base(1, 1, 0), cds.at[0], cpart)
-    for c in xrs + yrs + [zex] + yag + xag + [cag]:
+    for c in xrs + xag + [cag]:
         c.wait_send()
     for i in range(4):
         swap(i).wait_send()
@@ -465,7 +493,7 @@
         + [
             dma((n,))
             for n in (
-                1, 16, 1, 16, 1, 16, 1, 8, 1, 16, 1, 16, 1, 16,
+                32, 32, 32, 32, 1, 16, 1, 8, 1, 16, 1, 16, 1, 16,
                 3, 3, 3, 3, 1, 1, 3, 3, 3, 3, 1, 1, 4, 4, 4, 3, 4,
             )
         ],

time: 145 us -> 136 us (0.938); the launches traced: 144 us -> 133 us
  Pallas kernels: 141 us -> 130 us
    pallas_call x1, Pallas kernels: 141 us -> 130 us  [per_device(): pl.pallas_call(kernel, out_shape=jax.ShapeDtypeStruct((4, N, N), BF), in_...]
where the time goes in v1:
time: 136 us; the launch traced here: 133 us
  Pallas kernels  130 us (96%)
  local copies, waits for them, and re-layouts  3.05 us (2%)
    pallas_call x1, Pallas kernels, per_device(): pl.pallas_call(kernel, out_shape=jax.ShapeDtypeStruct((4, N, N), BF), in_...  130 us
    unnamed x1, local copies, waits for them, and re-layouts  3.05 us

profile of v1, /device:TPU:33, one launch (start us, length us, event | category | flops | bytes accessed | tf_op | source)
XLA Modules:
  0.0 133.0 jit_solution(6070399552045670888)
XLA Ops:
  0.0 129.9 %afno.1 = bf16[4,512,512]{2,1,0:T(8,128)(2,1)} custom-call(bf16[4,512,512]{2,1,0:T(8,128)(2,1)} %f_hbm.1, f32[256]{0:T(256)} %gain.1, f32[256]{0:T(256)} %shift.1, bf16[2,8,32,32]{3,2,1,0:T(8,128)(2,1)} %w1.1, bf16[2,8,32,32]{3,2,1,0:T(8,128)(2,1)} %w2.1, f32[2,256]{1,0:T(2,128)} %bias.1, bf16[2,512,256]{2,1,0:T(8,128)(2,1)} %constant.6.clone.fwd_hbm, ...), custom_call_target="tpu_custom_call" | custom-call | tf_op jit(solution)/shard_map/afno/pallas_call | solution.py:463
  129.9 3.0 %copy.11 = bf16[4,512,512]{2,1,0:T(8,128)(2,1)} copy(bf16[4,512,512]{2,1,0:T(8,128)(2,1)} %afno.1) | data formatting | bytes 4194304

commit v2 on v1

v2 whole, which is shorter than its diff:
```python
import functools
import math

import jax
import jax.numpy as jnp
import ml_dtypes
import numpy as np
from jax import lax
from jax.experimental import pallas as pl
from jax.experimental.pallas import tpu as pltpu
from jax.sharding import PartitionSpec as P

MESH = pl.DeviceIdType.MESH
BF = jnp.bfloat16
F32 = jnp.float32
N = 512
ROWS = 128
SS = 136
KB = 64
BAND = 128
ZA = 9
YB = 4
YA = 2
FZ = 4
YM = (3, 5, 7, 9)


def tables():
    half = N // 2
    idx = np.arange(N)
    step = np.float32(2.0 * math.pi / N)
    scale = np.float32(1.0 / math.sqrt(N))
    angle_w = ((idx[:, None] * np.arange(half)[None, :]) % N).astype(np.float32) * step
    cos_w, sin_w = np.cos(angle_w), np.sin(angle_w)
    weight = np.where(np.arange(half) == 0, 1.0, 2.0).astype(np.float32)
    re, im = cos_w * scale, -sin_w * scale
    fwd = np.stack(
        [np.concatenate([re[:, s], im[:, s]], 1) for s in (slice(0, 128), slice(128, 256))]
    )
    ire, iim = (cos_w * weight * scale).T, (-sin_w * weight * scale).T
    inv = np.stack(
        [np.concatenate([ire[s], iim[s]], 0) for s in (slice(0, 128), slice(128, 256))]
    )
    angle_h = ((idx[:, None] * idx[None, :]) % N).astype(np.float32) * step
    both = np.concatenate([np.cos(angle_h) * scale, np.sin(angle_h) * scale], 1)
    cast = lambda a: a.astype(ml_dtypes.bfloat16)
    return cast(fwd), cast(inv), cast(both)


def kernel(
    f_hbm, gain, shift, w1, w2, bias, fwd_hbm, inv_hbm, both_hbm,
    out_hbm,
    fld, modes, stage, shr_re, shr_im, acc, stat, part, xbuf, xsum, ybuf, ysum, zbuf,
    fwd_t, inv_t, both_t, big1, big2, bcol, stack, back_out, back_in, out_v,
    zs, zr, ys, yr, ds, dr, os, orr, cys, cyr, czs, czr, cds, cdr,
    zms, zmr, yms, ymr, dms, dmr,
    xs1, xr1, ys1, yr1, zs1, zr1, ys2, yr2, xs2, xr2, cs2, cr2, bs, br, loc, tab, outs,
):
    b = lax.axis_index("batch")
    g = lax.axis_index("grid")
    core = lax.rem(g, 2)
    zh = lax.rem(lax.div(g, 2), 2)
    y = lax.rem(lax.div(g, 4), 4)
    x = lax.div(g, 16)
    yy = lax.rem(y, 2)
    blk = lax.div(g, 8)

    def dev(x_, y_, z_, c_):
        return (b, ((x_ * 4 + y_) * 2 + z_) * 2 + c_)

    def flip(v, d):
        return v + d - 2 * v * d

    def chip(dy, dz):
        return flip(yy, dy) * 2 + flip(zh, dz)

    def base(dy, dz, dc):
        return (chip(dy, dz) * 2 + flip(core, dc)) * 4

    ypart = dev(x, y + 1 - 2 * yy, zh, core)
    zpart = dev(x, y, 1 - zh, core)
    cpart = dev(x, y, zh, 1 - core)
    xpeer = [lax.rem(x + 4 - d, 4) for d in (1, 2, 3)]
    ypeer = [lax.rem(y + 4 - d, 4) for d in (1, 2, 3)]
    xdev = [dev(v, y, zh, core) for v in xpeer]
    ydev = [dev(x, v, zh, core) for v in ypeer]

    def remote(src, dst, send, recv, to):
        return pltpu.make_async_remote_copy(
            src_ref=src, dst_ref=dst, send_sem=send, recv_sem=recv, device_id=to, device_id_type=MESH
        )

    own = base(0, 0, 0)
    tabs = [
        pltpu.make_async_copy(fwd_hbm.at[core], fwd_t, tab.at[0]),
        pltpu.make_async_copy(inv_hbm, inv_t, tab.at[1]),
        pltpu.make_async_copy(both_hbm, both_t, tab.at[2]),
    ]
    fetch = [pltpu.make_async_copy(f_hbm.at[i], fld.at[own + i], loc.at[i]) for i in range(4)]
    for c in fetch:
        c.start()

    barrier = pltpu.get_barrier_semaphore()
    peers = xdev + ydev + [zpart, cpart]
    for p in peers:
        pl.semaphore_signal(barrier, inc=1, device_id=p, device_id_type=MESH)
    pl.semaphore_wait(barrier, len(peers))
    for c in fetch:
        c.wait()
    for c in tabs:
        c.start()

    def rows_at(first, n, size):
        per = N // size
        row = pl.multiple_of((n % per) * size, size)
        return fld.at[first + n // per, pl.ds(row, size), :]

    def same(ref, send, recv, to):
        return remote(ref, ref, send, recv, to)

    def zchunk(n):
        return same(rows_at(own, n, 64), zs.at[n], zr.at[n], zpart)

    def ychunk(n):
        return same(rows_at(own, n, 64), ys.at[n], yr.at[n], ypart)

    def dchunk(n):
        return same(rows_at(base(0, 1, 0), n, 128), ds.at[0], dr.at[n], ypart)

    def cychunk(n):
        return same(rows_at(base(1, 0, 0), n, 128), cys.at[0], cyr.at[n], cpart)

    def czchunk(n):
        return same(rows_at(base(0, 1, 0), n, 128), czs.at[0], czr.at[n], cpart)

    def cdchunk(n):
        return same(rows_at(base(1, 1, 0), n, 128), cds.at[0], cdr.at[n], cpart)

    def mode_rows(c, n):
        return modes.at[c, 3, pl.ds(pl.multiple_of(n * 512, 512), 512), :]

    def zmode(n):
        return same(mode_rows(chip(0, 0), n), zms.at[n], zmr.at[n], zpart)

    def ymode(n):
        return same(mode_rows(chip(0, 0), n), yms.at[0], ymr.at[n], ypart)

    def dmode(n):
        return same(mode_rows(chip(0, 1), n), dms.at[0], dmr.at[n], ypart)

    def owncopy(i, h):
        rows = pl.ds(pl.multiple_of(256 * h, 256), 256)
        return fld.at[own + i, rows, :]

    def forward_z(n):
        zchunk(2 * n).wait_recv()
        zchunk(2 * n + 1).wait_recv()
        dchunk(n).start()
        czchunk(n).start()

    def forward_y(n):
        ychunk(2 * n).wait_recv()
        ychunk(2 * n + 1).wait_recv()
        cychunk(n).start()

    def forward_d(n):
        dchunk(n).wait_recv()
        cdchunk(n).start()

    ownc = [same(owncopy(i, 1 - core), os.at[0], orr.at[i], cpart) for i in range(4)]
    ownc += [same(owncopy(i, core), os.at[0], orr.at[4 + i], cpart) for i in range(4)]
    for c in ownc[:4]:
        c.start()

    def pump(chunk, first, last):
        for n in range(first, last):
            if n > 1:
                chunk(n - 2).wait_send()
            chunk(n).start()

    pump(zchunk, 0, 2)
    pump(ychunk, 0, 2)
    for c in ownc[4:]:
        c.start()

    for c in ownc[:4]:
        c.wait_recv()
    other = base(0, 0, 1)

    def partial_sums(r, _):
        row = pl.multiple_of(256 * core + r * 16, 16)
        s1 = jnp.zeros((16, N), F32)
        s2 = jnp.zeros((16, N), F32)
        for first in (own, other):
            for i in range(4):
                v = fld[first + i, pl.ds(row, 16), :].astype(F32)
                s1 = s1 + v
                s2 = s2 + v * v
        at = pl.ds(pl.multiple_of(r * 16, 16), 16)
        part[0, at, :] = s1
        part[1, at, :] = s2
        return 0

    lax.fori_loop(0, 16, partial_sums, 0)

    def part_rows(x_, y_):
        return pl.ds(pl.multiple_of(64 * x_ + 16 * y_, 16), 16)

    yown = ypeer + [y]
    xrs = [
        [
            remote(
                part.at[:, part_rows(xpeer[d], yown[p]), :],
                xbuf.at[d, p], xs1.at[d * 4 + p], xr1.at[d * 4 + p], xdev[d],
            )
            for d in range(3)
        ]
        for p in range(4)
    ]
    for c in sum(xrs, []):
        c.start()

    for c in tabs:
        c.wait()

    def iota(shape, dim):
        return lax.broadcasted_iota(jnp.int32, shape, dim)

    ch = iota((256, 32), 0)
    pick = (ch % 32 == iota((256, 32), 1)).astype(BF)
    ch_in = (ch // 64) * 8 + (ch % 2) * 4 + (ch // 16) % 4
    pick_in = (ch_in == iota((256, 32), 1)).astype(BF)
    nt = (((1,), (1,)), ((), ()))

    def expand(w, sel, cols):
        left = lax.dot_general(sel, w, nt, preferred_element_type=F32).astype(BF)
        return lax.dot_general(left, cols, nt, preferred_element_type=F32)

    def complex_matrix(rows, per, sel, w, cols, cpart_, ck):
        t0 = expand(w[0, blk], sel, cols)
        t1 = expand(w[1, blk], sel, cols)
        r = iota((rows, 256), 0)
        rp = r // (4 * per)
        hit = (r // per) % 4 == ck
        val = jnp.where(rp == cpart_, t0, jnp.where(rp == 1, t1, -t1))
        return jnp.where(hit, val, 0.0).astype(BF)

    c1 = iota((256, 256), 1)
    big1[...] = complex_matrix(256, 32, pick, w1, pick_in, (c1 // 2) % 2, (c1 // 4) % 4)
    pick2 = ((iota((64, 32), 0) % 8) + chip(0, 0) * 8 == iota((64, 32), 1)).astype(BF)
    c2 = iota((64, 256), 1)
    big2[...] = complex_matrix(64, 8, pick2, w2, pick, c2 // 128, (c2 // 32) % 4)
    r = iota((256, 256), 0)
    hit = (r % 32) + blk * 32 == c1
    value = jnp.where(r < 128, bias[0:1, :], bias[1:2, :])
    col = jnp.sum(jnp.where(hit, value, 0.0), axis=1, keepdims=True)
    bcol[...] = jnp.broadcast_to(col, (256, 128))

    def clear(i, _):
        acc[i] = jnp.zeros((N, 256), F32)
        return 0

    lax.fori_loop(0, 8, clear, 0)

    for n in range(2, ZA):
        pump(ychunk, 2 * n - 2, 2 * n)
        pump(zchunk, n, n + 1)
    yrs = [
        remote(xsum.at[p], ybuf.at[p], ys1.at[p], yr1.at[p], ydev[p]) for p in range(3)
    ]
    for p in range(4):
        for c in xrs[p]:
            c.wait_recv()
        xsum[p] = part[:, part_rows(x, yown[p]), :] + xbuf[0, p] + xbuf[1, p] + xbuf[2, p]
        if p < 3:
            yrs[p].start()
    for c in yrs:
        c.wait_send()
    pump(ychunk, 2 * ZA - 2, 2 * ZA + YA)
    pump(zchunk, ZA, ZA + 1)
    for c in yrs:
        c.wait_recv()
    ysum[...] = xsum[3] + ybuf[0] + ybuf[1] + ybuf[2]
    zex = remote(ysum, zbuf, zs1.at[0], zr1.at[0], zpart)
    zex.start()
    pump(ychunk, 2 * ZA + YA, 2 * ZA + YB)
    zex.wait_send()
    pump(zchunk, ZA + 1, ZA + 3)
    zex.wait_recv()
    total = ysum[...] + zbuf[...]
    mean = total[0] * (1.0 / 256.0)
    var = total[1] * (1.0 / 256.0) - mean * mean
    row0 = 256 * core

    def stat_rows(x_, y_):
        return stat.at[:, pl.ds(pl.multiple_of(row0 + 64 * x_ + 16 * y_, 16), 16), :]

    mine = pl.ds(pl.multiple_of(row0 + 64 * x + 16 * y, 16), 16)
    stat[0, mine, :] = mean
    stat[1, mine, :] = lax.rsqrt(var + 1e-5)
    yag = [same(stat_rows(x, y), ys2.at[d], yr2.at[d], ydev[d]) for d in range(3)]
    ygot = [same(stat_rows(x, ypeer[d]), ys2.at[d], yr2.at[2 - d], ydev[d]) for d in range(3)]
    xag = [
        [same(stat_rows(x, yown[p]), xs2.at[d * 4 + p], xr2.at[d * 4 + p], xdev[d]) for d in range(3)]
        for p in range(4)
    ]
    for c in yag + xag[3]:
        c.start()
    for c in yag:
        c.wait_send()
    pump(zchunk, ZA + 3, ZA + 4)
    for p in range(3):
        ygot[p].wait_recv()
        for c in xag[p]:
            c.start()

    def quarter(x_, d):
        rows = stat.at[:, pl.ds(pl.multiple_of(row0 + 64 * x_, 64), 64), :]
        return same(rows, cs2.at[d], cr2.at[d], cpart)

    cag = [quarter(v, d) for d, v in enumerate(xpeer + [x])]
    cag[3].start()
    for n in range(ZA + 4, 24):
        zchunk(n).start()
    for n in range(2 * ZA + YB, 24):
        ychunk(n).start()

    for n in range(7):
        if n < FZ:
            forward_z(n)
        forward_y(n)
    for d in range(3):
        for p in range(4):
            xag[p][2 - d].wait_recv()
        cag[d].start()
    for n in range(FZ, 7):
        forward_z(n)
    for n in range(7, 12):
        forward_y(n)
    for c in cag + ownc[4:]:
        c.wait_recv()

    def forward(slot, at):
        gn = gain[blk * 32 + slot]
        sh = shift[blk * 32 + slot]
        for h in range(0, N, 128):
            rows = slice(h, h + 128)
            v = fld[slot, rows, :].astype(F32)
            nrm = ((v - stat[0, rows, :]) * stat[1, rows, :] * gn + sh).astype(BF)
            a = jnp.dot(nrm, fwd_t[...], preferred_element_type=F32)
            stack[h : h + 128, :] = a.astype(BF)
            stack[N + h : N + h + 128, :] = jnp.concatenate([a[:, 128:], -a[:, :128]], 1).astype(BF)
        m = jnp.dot(both_t[...], stack[...], preferred_element_type=F32)
        stage[pl.ds(at, N, stride=4), :] = m[:, :128]
        stage[pl.ds(at + 2, N, stride=4), :] = m[:, 128:]

    def forward_mode(n):
        zmode(n).wait_recv()
        dmode(n).start()

    def unit(t, _):
        for at, n in ((2, 7), (4, 8), (7, 9), (9, 10), (11, 11)):

            @pl.when(t == at)
            def _(n=n):
                forward_z(n)

        for at, n in zip((10, 11), range(2)):

            @pl.when(t == at)
            def _(n=n):
                zmode(n).start()

        for at, n in zip(YM, range(4)):

            @pl.when(t == at)
            def _(n=n):
                ymode(n).start()

        @pl.when(t == 4)
        def _():
            for n in range(12):
                cychunk(n).wait_recv()

        @pl.when(t == 7)
        def _():
            for n in range(8):
                czchunk(n).wait_recv()

        @pl.when(t == 9)
        def _():
            for n in range(4):
                forward_d(n)
            for n in range(4):
                cdchunk(n).wait_recv()

        @pl.when(t == 10)
        def _():
            for n in range(4, 8):
                forward_d(n)
            for n in range(4, 8):
                cdchunk(n).wait_recv()

        @pl.when(t == 11)
        def _():
            for n in range(8, 12):
                czchunk(n).wait_recv()

        @pl.when(t == 12)
        def _():
            for n in range(8, 12):
                forward_d(n)
            zmode(0).wait_send()
            zmode(2).start()
            for n in range(8, 12):
                cdchunk(n).wait_recv()

        late = t > 10
        diag = t > 8
        dy = jnp.where(late, t - 11, jnp.where(diag, 1, jnp.where(t > 6, 0, jnp.where(t > 3, 1, 0))))
        dz = jnp.where(t > 6, 1, 0)
        i = jnp.where(
            late, 2,
            jnp.where(
                diag, t - 9,
                jnp.where(t > 6, t - 7, jnp.where(t > 3, t - 4, jnp.where(t == 0, 3, t - 1))),
            ),
        )
        c = chip(dy, dz)

        def one(e, _):
            forward(c * 8 + e * 4 + i, e)
            return 0

        lax.fori_loop(0, 2, one, 0)
        modes[c, i] = stage[...].astype(BF)

        return 0

    lax.fori_loop(0, 13, unit, 0)
    forward_mode(0)
    zmode(1).wait_send()
    zmode(3).start()

    groups = KB // 4

    def mix(t, k0):
        cols = []
        for q in range(groups):
            at = pl.ds(pl.multiple_of((k0 + t * KB + q * 4) * 4, 16), 16)
            cols.append(jnp.concatenate([modes[j, i, at, :] for j in range(4) for i in range(4)], 0))
        z = jnp.concatenate(cols, 1)
        hid = jnp.dot(big1[...], z, preferred_element_type=F32)
        hid = jnp.maximum(hid + jnp.concatenate([bcol[...]] * groups, 1), 0.0).astype(BF)
        o = jnp.dot(big2[...], hid, preferred_element_type=F32)
        o = jnp.maximum(o - 0.01, 0.0) + jnp.minimum(o + 0.01, 0.0)
        for q in range(groups):
            for k in range(4):
                at = pl.ds(t * KB + q * 4 + k, 8, stride=SS)
                shr_re[at, :] = o[k * 8 : k * 8 + 8, q * 128 : q * 128 + 128]
                shr_im[at, :] = o[32 + k * 8 : 40 + k * 8, q * 128 : q * 128 + 128]
        return k0

    def band(t, _):
        @pl.when(t < 3)
        def _():
            forward_mode(t + 1)

        ymode(t).wait_recv()
        dmode(t).wait_recv()
        k0 = pl.multiple_of(t * BAND, BAND)
        lax.fori_loop(0, BAND // KB, mix, k0)

        left = jnp.concatenate(
            [both_t[:, pl.ds(k0, BAND)], both_t[:, pl.ds(pl.multiple_of(N + k0, BAND), BAND)]], 1
        )

        def backward(c8, _):
            at = pl.ds(pl.multiple_of(c8 * SS, 8), BAND)
            sr, si = shr_re[at, :], shr_im[at, :]
            right = jnp.concatenate(
                [jnp.concatenate([sr, si], 1), jnp.concatenate([-si, sr], 1)], 0
            ).astype(BF)
            acc[c8] = acc[c8] + jnp.dot(left, right, preferred_element_type=F32)
            return 0

        lax.fori_loop(0, 8, backward, 0, unroll=4)
        return 0

    lax.fori_loop(0, N // BAND, band, 0)

    def swap(i):
        return remote(back_out.at[i], back_in.at[i], bs.at[i], br.at[i], cpart)

    def give(i, _):
        back_out[i] = acc[(1 - core) * 4 + i].astype(BF)
        swap(i).start()
        return 0

    def put(i):
        return pltpu.make_async_copy(out_v.at[i], out_hbm.at[i], outs.at[i])

    def finish(i, _):
        filt = jnp.dot(acc[core * 4 + i].astype(BF), inv_t[core], preferred_element_type=F32)
        swap(i).wait_recv()
        filt = filt + jnp.dot(back_in[i], inv_t[1 - core], preferred_element_type=F32)
        out_v[i] = (fld[own + i].astype(F32) + filt).astype(BF)
        put(i).start()
        return 0

    lax.fori_loop(0, 4, give, 0)
    lax.fori_loop(0, 4, finish, 0)

    for n in range(ZA + 2, 24):
        zchunk(n).wait_send()
    for n in range(2 * ZA + YB - 2, 24):
        ychunk(n).wait_send()

    def drain(ref, send, to):
        same(ref, send, zr.at[0], to).wait_send()

    def raw(first):
        return fld.at[pl.ds(first, 3)]

    drain(fld.at[pl.ds(own, 4)], os.at[0], cpart)
    drain(raw(base(0, 1, 0)), ds.at[0], ypart)
    drain(raw(base(1, 0, 0)), cys.at[0], cpart)
    drain(raw(base(0, 1, 0)), czs.at[0], cpart)
    drain(raw(base(1, 1, 0)), cds.at[0], cpart)
    for n in range(2, 4):
        zmode(n).wait_send()
    drain(modes.at[chip(0, 0), 3], yms.at[0], ypart)
    drain(modes.at[chip(0, 1), 3], dms.at[0], ypart)
    for c in sum(xrs, []) + sum(xag, []) + cag:
        c.wait_send()
    for i in range(4):
        swap(i).wait_send()
        put(i).wait()


def per_device(fields, norm_gain, norm_shift, first_weight, second_weight, first_bias):
    fwd, inv, both = tables()
    dma = pltpu.SemaphoreType.DMA
    vm, sm, hbm = pltpu.VMEM, pltpu.SMEM, pl.ANY
    spec = lambda s: pl.BlockSpec(memory_space=s)
    return pl.pallas_call(
        kernel,
        out_shape=jax.ShapeDtypeStruct((4, N, N), BF),
        in_specs=[spec(s) for s in (hbm, sm, sm, vm, vm, vm, hbm, hbm, hbm)],
        out_specs=spec(hbm),
        scratch_shapes=[
            vm((32, N, N), BF),
            vm((4, 4, 4 * N, 128), BF),
            vm((4 * N, 128), F32),
            vm((8 * SS, 128), F32),
            vm((8 * SS, 128), F32),
            vm((8, N, 256), F32),
            vm((2, N, N), F32),
            vm((2, 256, N), F32),
            vm((3, 4, 2, 16, N), F32),
            vm((4, 2, 16, N), F32),
            vm((3, 2, 16, N), F32),
            vm((2, 16, N), F32),
            vm((2, 16, N), F32),
            vm((N, 256), BF),
            vm((2, 256, N), BF),
            vm((N, 2 * N), BF),
            vm((256, 256), BF),
            vm((64, 256), BF),
            vm((256, 128), F32),
            vm((2 * N, 256), BF),
            vm((4, N, 256), BF),
            vm((4, N, 256), BF),
            vm((4, N, N), BF),
        ]
        + [
            dma((n,))
            for n in (
                24, 24, 24, 24, 1, 12, 1, 8, 1, 12, 1, 12, 1, 12,
                4, 4, 1, 4, 1, 4,
                12, 12, 3, 3, 1, 1, 3, 3, 12, 12, 4, 4, 4, 4, 4, 3, 4,
            )
        ],
        compiler_params=pltpu.CompilerParams(
            collective_id=0, has_side_effects=True, vmem_limit_bytes=67043328
        ),
        name="afno",
    )(fields, norm_gain, norm_shift, first_weight, second_weight, first_bias, fwd, inv, both)


def solution(mesh):
    return jax.shard_map(
        per_device,
        mesh=mesh,
        in_specs=(P(("batch", "grid"), None, None), P(), P(), P(), P(), P()),
        out_specs=P(("batch", "grid"), None, None),
        check_vma=False,
    )
```

time: 136 us -> 131 us (0.963); the launches traced: 133 us -> 130 us
  Pallas kernels: 130 us -> 127 us
    pallas_call x1, Pallas kernels: 130 us -> 127 us  [per_device(): pl.pallas_call(kernel, out_shape=jax.ShapeDtypeStruct((4, N, N), BF), in_...]
where the time goes in v2:
time: 131 us; the launch traced here: 130 us
  Pallas kernels  127 us (97%)
  local copies, waits for them, and re-layouts  3.05 us (2%)
    pallas_call x1, Pallas kernels, per_device(): pl.pallas_call(kernel, out_shape=jax.ShapeDtypeStruct((4, N, N), BF), in_...  127 us
    unnamed x1, local copies, waits for them, and re-layouts  3.05 us

profile of v2, /device:TPU:33, one launch (start us, length us, event | category | flops | bytes accessed | tf_op | source)
XLA Modules:
  0.0 129.6 jit_solution(14071157273147774646)
XLA Ops:
  0.0 126.6 %afno.1 = bf16[4,512,512]{2,1,0:T(8,128)(2,1)} custom-call(bf16[4,512,512]{2,1,0:T(8,128)(2,1)} %f_hbm.1, f32[256]{0:T(256)} %gain.1, f32[256]{0:T(256)} %shift.1, bf16[2,8,32,32]{3,2,1,0:T(8,128)(2,1)} %w1.1, bf16[2,8,32,32]{3,2,1,0:T(8,128)(2,1)} %w2.1, f32[2,256]{1,0:T(2,128)} %bias.1, bf16[2,512,256]{2,1,0:T(8,128)(2,1)} %constant.6.clone.fwd_hbm, ...), custom_call_target="tpu_custom_call" | custom-call | tf_op jit(solution)/shard_map/afno/pallas_call | solution.py:546
  126.6 3.0 %copy.11 = bf16[4,512,512]{2,1,0:T(8,128)(2,1)} copy(bf16[4,512,512]{2,1,0:T(8,128)(2,1)} %afno.1) | data formatting | bytes 4194304
